TPU v7x, 32 devices: a whole 2x2x4 slice. The times are simulated.
32 devices in a mesh: groups: 1, slab: 8 (over z, y), coil: 2 (over x), row: 2 (over core).
Axes of the slice: x: 2, y: 2, z: 4, core: 2. Of those that a mesh axis runs over, the one named last changes fastest.
Arguments:
- image: float32 [2, 128, 256, 128], P('groups', None, ('slab', 'row')), may hold values from -6 to 6
- sens: bfloat16 [2, 16, 128, 256, 128], P('groups', 'coil', None, ('slab', 'row')), may hold values from -1.5 to 1.5
- measured: bfloat16 [2, 16, 128, 256, 128], P('groups', 'coil', ('slab', 'row')), may hold values from -3 to 3
- mask: int32 [128, 256], P(('slab', 'row')), may hold values from 0 to 1, as said below
- thresholds: float32 [2, 7], replicated, may hold values from 0.1 to 1.5
Outputs:
- image_next: float32 [2, 128, 256, 128], P('groups', None, ('slab', 'row'))
Inputs may be any that keep to these rules, and one draw needn't show every extreme that they name: `mask`: A calibration block of the 8 central phase-encode lines (ky from 60 to 67) is sampled at every kz; outside it each (ky, kz) is sampled independently at random.
All inputs are finite; a program needn't handle non-finite values.
Results may differ from a plain program's by a relative error of at most 0.013.
Values may be sent and summed in bfloat16 or wider, within the bound.
A program may use at most 128 MiB of HBM per device.

v0:
```python
import math
import jax
import jax.numpy as jnp
from jax import lax
from jax.sharding import PartitionSpec as P

half_root = 0.7071067811865476
quarter_root = 0.3535533905932738
step_size = 0.5


def passed_along(block, axis, distance):
    devices = range(lax.axis_size(axis))
    route = [((i - distance) % len(devices), i) for i in devices]
    return lax.ppermute(block, axis, route)


def fourier_table(length, sign):
    index = jnp.arange(length, dtype=jnp.int32)
    phase = index[:, None] * index[None, :] % length
    theta = phase.astype(jnp.float32) * jnp.float32(2.0 * math.pi / length)
    scale = jnp.float32(1.0 / math.sqrt(length))
    real = jnp.cos(theta) * scale
    imaginary = jnp.sin(theta) * (sign * scale)
    upper = jnp.stack([real, -imaginary])
    lower = jnp.stack([imaginary, real])
    return jnp.stack([upper, lower]).astype(jnp.bfloat16)


def contract(form, values, table):
    return jnp.einsum(form, values, table, preferred_element_type=jnp.float32)


def complex_product(left, right):
    return jnp.stack(
        [left[0] * right[0] - left[1] * right[1], left[0] * right[1] + left[1] * right[0]]
    )


def roll_after(values, along, offset):
    return jnp.roll(values, -offset, axis=along)


def roll_before(values, along, offset):
    return jnp.roll(values, offset, axis=along)


def plane_after(values, along, offset):
    border = lax.slice_in_dim(values, 0, offset, axis=along)
    fetched = passed_along(border.astype(jnp.bfloat16), ("slab", "row"), -1).astype(border.dtype)
    remain = lax.slice_in_dim(values, offset, values.shape[along], axis=along)
    return jnp.concatenate([remain, fetched], axis=along)


def plane_before(values, along, offset):
    extent = values.shape[along]
    border = lax.slice_in_dim(values, extent - offset, extent, axis=along)
    fetched = passed_along(border.astype(jnp.bfloat16), ("slab", "row"), 1).astype(border.dtype)
    remain = lax.slice_in_dim(values, 0, extent - offset, axis=along)
    return jnp.concatenate([fetched, remain], axis=along)


def split_bands(bands, along, offset, after):
    moved = after(bands, along, offset)
    return jnp.concatenate([(bands + moved) * half_root, (bands - moved) * half_root], axis=0)


def merge_bands(bands, along, offset, before):
    half = bands.shape[0] // 2
    lower = bands[:half]
    upper = bands[half:]
    return (lower + upper + before(lower - upper, along, offset)) * quarter_root


def shrink_detail(detail, limit):
    magnitude = jnp.sqrt(detail[:, 0] * detail[:, 0] + detail[:, 1] * detail[:, 1])
    limit = limit.reshape((-1, 1, 1, 1))
    factor = jnp.maximum(magnitude - limit, 0.0) / jnp.maximum(magnitude, limit)
    return detail * factor[:, None]


def wavelet_shrink(descent, thresholds, moves):
    coarse = descent[None]
    details = []
    for level in range(thresholds.shape[0]):
        offset = 2**level
        bands = coarse
        for along, after, before in moves:
            bands = split_bands(bands, along, offset, after)
        coarse = bands[:1]
        details.append(shrink_detail(bands[1:], thresholds[level]))
    for level in reversed(range(thresholds.shape[0])):
        offset = 2**level
        bands = jnp.concatenate([coarse, details[level]], axis=0)
        for along, after, before in reversed(moves):
            bands = merge_bands(bands, along, offset, before)
        coarse = bands
    return coarse[0]


def local(image, sens, measured, mask, thresholds):
    readout_cells = image.shape[3]
    phase_cells = image.shape[1]
    depth_cells = measured.shape[3]
    table_readout = fourier_table(readout_cells, -1.0)
    table_phase = fourier_table(phase_cells, -1.0)
    table_depth = fourier_table(depth_cells, -1.0)
    inverse_readout = fourier_table(readout_cells, 1.0)
    inverse_phase = fourier_table(phase_cells, 1.0)
    inverse_depth = fourier_table(depth_cells, 1.0)
    sens_wide = sens.astype(jnp.float32)
    coil_image = complex_product(sens_wide, image[:, None]).astype(jnp.bfloat16)
    readout_done = contract("tcyzj,stjk->scyzk", coil_image, table_readout).astype(jnp.bfloat16)
    phase_done = contract("tcjzx,stjk->sckzx", readout_done, table_phase).astype(jnp.bfloat16)
    spread = lax.all_to_all(phase_done, ("slab", "row"), split_axis=2, concat_axis=3, tiled=True)
    spectrum = contract("tcyjx,stjk->scykx", spread, table_depth)
    sampled = mask.astype(jnp.float32)[None, None, :, :, None]
    residual = (sampled * (spectrum - measured.astype(jnp.float32))).astype(jnp.bfloat16)
    depth_back = contract("tcyjx,stjk->scykx", residual, inverse_depth).astype(jnp.bfloat16)
    gathered = lax.all_to_all(depth_back, ("slab", "row"), split_axis=3, concat_axis=2, tiled=True)
    phase_back = contract("tcjzx,stjk->sckzx", gathered, inverse_phase).astype(jnp.bfloat16)
    readout_back = contract("tcyzj,stjk->scyzk", phase_back, inverse_readout)
    partial_value = jnp.stack(
        [
            jnp.sum(sens_wide[0] * readout_back[0] + sens_wide[1] * readout_back[1], axis=0),
            jnp.sum(sens_wide[0] * readout_back[1] - sens_wide[1] * readout_back[0], axis=0),
        ]
    )
    gradient = lax.psum(partial_value.astype(jnp.bfloat16), "coil").astype(jnp.float32)
    descent = image - step_size * gradient
    moves = [
        (4, roll_after, roll_before),
        (2, roll_after, roll_before),
        (3, plane_after, plane_before),
    ]
    return wavelet_shrink(descent, thresholds, moves)


def solution(mesh):
    return jax.shard_map(
        local,
        mesh=mesh,
        in_specs=(
            P("groups", None, ("slab", "row"), None),
            P("groups", "coil", None, ("slab", "row"), None),
            P("groups", "coil", ("slab", "row"), None, None),
            P(("slab", "row"), None),
            P(),
        ),
        out_specs=P("groups", None, ("slab", "row"), None),
        check_vma=False,
    )
```

profile of v0, /device:TPU:0, one launch (start us, length us, event | category | flops | bytes accessed | tf_op | source)
XLA Modules:
  0.0 727.4 jit_solution(10082498368846165496)
XLA Ops:
  7.4 11.7 %copy_convert_fusion = f32[2,8,128,16,128]{4,2,0,3,1:T(8,128)} fusion(bf16[2,8,128,16,128]{4,3,2,1,0:T(8,128)(2,1)} %param.6), kind=kLoop, calls=%fused_computation.53 | loop fusion | flops 4194304 | bytes 25165824 | tf_op jit(solution)/shard_map/convert_element_type | solution.py:111
  19.3 0.3 copy.36
  19.6 0.3 copy.35
  20.0 9.9 %subtract_convert_fusion = (bf16[1,8,128,16,128]{4,2,0,3,1:T(8,128)(2,1)}, bf16[1,8,128,16,128]{4,2,0,3,1:T(8,128)(2,1)}) fusion(f32[2,8,128,16,128]{4,2,0,3,1:T(8,128)} %copy_convert_fusion, f32[128,16,128]{2,0,1:T(8,128)S(1)} %copy.36, f32[128,16,128]{2,0,1:T(8,128)S(1)} %copy.35), kind=kLoop, calls=%fused_computation.61 | loop fusion | flops 16777216 | bytes 27262976 | tf_op jit(solution)/shard_map/convert.8
  29.9 9.1 %fusion.6 = bf16[2,8,128,16,128]{4,2,3,1,0:T(8,128)(2,1)} fusion(bf16[1,8,128,16,128]{4,2,0,3,1:T(8,128)(2,1)} %get-tuple-element.8, bf16[1,8,128,16,128]{4,2,0,3,1:T(8,128)(2,1)} %get-tuple-element.7, bf16[1,2,128,128]{2,3,1,0:T(8,128)(2,1)S(1)} %get-tuple-element.28, bf16[1,2,128,128]{2,3,1,0:T(8,128)(2,1)S(1)} %get-tuple-element.29), kind=kOutput, calls=%fused_computation.30 | convolution fusion | flops 4320657408 | bytes 16908288 | tf_op jit(solution)/shard_map/tcjzx,stjk->sckzx/dot_general | solution.py:31
  39.0 12.0 %copy.38 = bf16[2,8,128,16,128]{4,3,1,0,2:T(8,128)(2,1)} copy(bf16[2,8,128,16,128]{4,2,3,1,0:T(8,128)(2,1)} %fusion.6) | data formatting | bytes 16777216 | tf_op jit(solution)/shard_map/convert_element_type | solution.py:114
  51.0 7.6 %all-to-all-start = ((bf16[2,8,128,16,128]{4,3,1,0,2:T(8,128)(2,1)}), bf16[2,8,128,16,128]{4,3,1,0,2:T(8,128)(2,1)}, u32[]{:S(2)}, u32[]{:S(2)}) async-start(bf16[2,8,128,16,128]{4,3,1,0,2:T(8,128)(2,1)} %copy.38), calls=%async_computation | async-start | bytes 16777216 | tf_op jit(solution)/shard_map/all_to_all | solution.py:115
  58.7 1.0 multiply_convert_fusion.2
  59.7 1.3 multiply_convert_fusion
  60.9 1.0 negate_convert_fusion
  62.0 147.1 %all-to-all-done = bf16[2,8,128,16,128]{4,3,1,0,2:T(8,128)(2,1)} async-done(((bf16[2,8,128,16,128]{4,3,1,0,2:T(8,128)(2,1)}), bf16[2,8,128,16,128]{4,3,1,0,2:T(8,128)(2,1)}, u32[]{:S(2)}, u32[]{:S(2)}) %all-to-all-start) | async-done | bytes 8388640 | tf_op jit(solution)/shard_map/all_to_all | solution.py:115
  209.2 9.1 %copy.40 = bf16[2,8,8,16,16,128]{5,4,3,2,1,0:T(8,128)(2,1)} copy(bf16[2,8,8,16,16,128]{5,4,1,0,2,3:T(8,128)(2,1)} %bitcast.31) | data formatting | bytes 16777216 | tf_op jit(solution)/shard_map/all_to_all | solution.py:115
  218.3 9.5 %fusion.1 = bf16[2,8,8,256,128]{4,3,2,1,0:T(8,128)(2,1)S(1)} fusion(bf16[2,8,8,256,128]{4,3,2,1,0:T(8,128)(2,1)} %param.7, f32[8,256]{1,0:T(8,128)S(1)} %convert_element_type.150, bf16[2,8,8,256,128]{4,3,2,1,0:T(8,128)(2,1)} %bitcast.172, bf16[1,2,256,256]{2,3,1,0:T(8,128)(2,1)S(1)} %get-tuple-element.24, bf16[1,2,256,256]{2,3,1,0:T(8,128)(2,1)S(1)} %get-tuple-element.25), kind=kOutput, calls=%fused_computation.10 | convolution fusion | flops 4312793088 | bytes 25698304 | tf_op jit(solution)/shard_map/tcyjx,stjk->scykx/dot_general | solution.py:31
  227.9 6.7 fusion.7
  234.6 12.1 %copy.43 = bf16[2,8,8,256,128]{4,2,1,0,3:T(8,128)(2,1)} copy(bf16[2,8,8,256,128]{4,3,2,1,0:T(8,128)(2,1)} %fusion.7) | data formatting | bytes 16777216 | tf_op jit(solution)/shard_map/convert_element_type | solution.py:119
  246.6 218.8 %all_to_all.36 = bf16[2,8,8,256,128]{4,2,1,0,3:T(8,128)(2,1)} all-to-all(bf16[2,8,8,256,128]{4,2,1,0,3:T(8,128)(2,1)} %copy.43), channel_id=1, replica_groups=mesh['groups'=1,'slab'=8,'coil'=2,'row'=2] {'slab','row'}, dimensions={3} | all-to-all | bytes 16777216 | tf_op jit(solution)/shard_map/all_to_all | solution.py:120
  465.4 16.3 %copy.45 = bf16[2,8,16,8,16,128]{5,4,3,2,1,0:T(8,128)(2,1)} copy(bf16[2,8,16,8,16,128]{5,3,1,0,4,2:T(8,128)(2,1)} %bitcast.169) | data formatting | bytes 16777216 | tf_op jit(solution)/shard_map/all_to_all | solution.py:120
  481.8 12.5 %convolution_bitcast_fusion = f32[2,8,128,16,128]{4,2,0,3,1:T(8,128)} fusion(bf16[2,8,128,16,128,1]{4,3,2,1,0,5:T(8,128)(2,1)} %bitcast.168, bf16[1,2,128,128]{2,3,1,0:T(8,128)(2,1)S(1)} %get-tuple-element.30, bf16[1,2,128,128]{2,3,1,0:T(8,128)(2,1)S(1)} %get-tuple-element.27), kind=kOutput, calls=%fused_computation.29 | convolution fusion | flops 4299685888 | bytes 25296896 | tf_op jit(solution)/shard_map/tcyzj,stjk->scyzk/dot_general | solution.py:31
  494.3 13.1 %add_reduce_fusion = (bf16[128,16,128]{2,0,1:T(8,128)(2,1)S(1)}, bf16[128,16,128]{2,0,1:T(8,128)(2,1)S(1)}) fusion(f32[2,8,128,16,128]{4,2,0,3,1:T(8,128)} %convolution_bitcast_fusion, f32[2,8,128,16,128]{4,2,0,3,1:T(8,128)} %copy_convert_fusion), kind=kLoop, calls=%fused_computation.59 | loop fusion | flops 16252928 | bytes 34603008 | tf_op jit(solution)/shard_map/reduce_sum | solution.py:125
  508.0 1.1 pad_maximum_fusion.14
  509.1 2.0 copy.50
  511.1 39.3 %all-reduce.2.cloned.1.call-done = bf16[2,128,16,128]{1,3,2,0:T(8,128)(2,1)} async-done(((bf16[2,128,16,128]{1,3,2,0:T(8,128)(2,1)}), bf16[2,128,16,128]{1,3,2,0:T(8,128)(2,1)}) %all-reduce.2.cloned.1.call-update) | async-done | bytes 1048592 | tf_op jit(solution)/shard_map/psum | solution.py:129
  550.4 1.6 fusion.55
  552.3 0.6 multiply_bitcast_fusion.1
  552.9 0.5 fusion.43
  553.4 1.1 fusion.42
  554.6 1.9 add_multiply_fusion.3
  556.6 3.6 collective-permute-start
  560.1 3.8 fusion.22
  564.1 6.8 subtract_multiply_fusion
  571.2 0.5 add_multiply_fusion.4
  571.7 3.0 fusion.41
  574.7 4.0 fusion.40
  578.7 4.2 subtract_multiply_fusion.2
  583.0 4.7 collective-permute-start.1
  587.7 5.4 divide_bitcast_fusion
  593.1 3.1 fusion.23
  596.3 8.9 %subtract_multiply_fusion.1 = (f32[4,2,128,16,128]{2,4,3,1,0:T(8,128)}, f32[4,2,128,16,128]{2,4,3,1,0:T(8,128)S(1)}) fusion(f32[4,2,128,2,128]{2,4,3,1,0:T(8,128)S(1)} %convert_element_type.163, f32[4,2,128,14,128]{2,4,3,1,0:T(8,128)} %fusion.23, f32[2,2,128,16,128]{2,4,3,1,0:T(8,128)} %copy-done.4, f32[2,2,128,16,128]{2,4,3,1,0:T(8,128)} %copy-done.5), kind=kLoop, calls=%fused_computation.55 | loop fusion | flops 12582912 | bytes 33554432 | tf_op jit(solution)/shard_map/mul | solution.py:65
  605.5 3.0 copy-done.1
  608.4 7.7 %divide_bitcast_fusion.1 = f32[7,128,16,128]{1,3,2,0:T(8,128)} fusion(f32[4,2,128,16,128]{2,4,3,1,0:T(8,128)} %get-tuple-element.9, f32[4,2,128,16,128]{2,4,3,1,0:T(8,128)S(1)} %get-tuple-element.10, f32[7]{0:T(128)S(1)} %get-tuple-element.31), kind=kLoop, calls=%fused_computation.79 | loop fusion | flops 16515072 | bytes 24117276 | tf_op jit(solution)/shard_map/mul | solution.py:79
  616.2 8.2 %fusion.5 = f32[7,2,128,16,128]{2,4,3,1,0:T(8,128)S(1)} fusion(f32[4,2,128,16,128]{2,4,3,1,0:T(8,128)} %copy-done.1, f32[4,2,128,16,128]{2,4,3,1,0:T(8,128)} %get-tuple-element.9, f32[7,128,16,128]{1,3,2,0:T(8,128)} %divide_bitcast_fusion.1), kind=kLoop, calls=%fused_computation.18 | loop fusion | flops 7340032 | bytes 38797312 | tf_op jit(solution)/shard_map/mul | solution.py:79
  624.4 4.0 slice_subtract_fusion.1
  628.4 1.3 slice.450
  629.8 11.4 %fusion.3 = f32[7,2,128,16,128]{2,4,3,1,0:T(8,128)} fusion(f32[4,2,128,16,128]{2,4,3,1,0:T(8,128)S(1)} %bitcast.165, f32[4,2,128,16,128]{2,4,3,1,0:T(8,128)} %copy-done.3, f32[7,128,16,128]{1,3,2,0:T(8,128)} %divide_bitcast_fusion), kind=kLoop, calls=%fused_computation.16 | loop fusion | flops 7340032 | bytes 38797312 | tf_op jit(solution)/shard_map/mul | solution.py:79
  641.3 6.9 slice.282
  648.3 6.9 fusion.10
  655.2 4.2 slice_subtract_fusion.3
  659.4 3.2 slice.285
  662.7 9.9 %fusion.44 = f32[2,2,128,16,128]{2,4,3,1,0:T(8,128)} fusion(f32[2,2,126,16,128]{2,4,3,1,0:T(8,128)} %bitcast.166, f32[2,2,2,16,128]{2,4,3,1,0:T(8,128)} %slice.285, f32[4,2,128,16,128]{2,4,3,1,0:T(8,128)} %fusion.10), kind=kLoop, calls=%fused_computation.97 | loop fusion | flops 4194304 | bytes 16777216 | tf_op jit(solution)/shard_map/mul | solution.py:72
  672.6 2.6 slice_subtract_fusion.5
  675.3 2.9 fusion.50
  678.2 1.8 slice_subtract_fusion
  680.1 3.3 copy-done.10
  683.5 7.3 %slice.297 = f32[4,2,128,15,128]{2,4,3,1,0:T(8,128)} slice(f32[4,2,128,16,128]{2,4,3,1,0:T(8,128)} %copy-done.10), slice={[0:4], [0:2], [0:128], [0:15], [0:128]} | slice | bytes 15728640 | tf_op jit(solution)/shard_map/slice | solution.py:59
  690.8 1.1 collective-permute-done.3
  692.0 7.2 fusion.11
  699.2 4.2 slice_subtract_fusion.2
  703.4 3.3 slice.300
  706.7 1.6 copy-done.2
  708.3 5.7 fusion.45
  714.0 2.6 slice_subtract_fusion.4
  716.7 0.8 copy-done.9
  717.5 0.9 fusion.52
  718.3 2.0 copy.52
  (71 shorter events, 3.2 us)
Async XLA Ops:
  7.4 11.7 %copy-start.11 = (f32[2,128,16,128]{3,2,1,0:T(8,128)S(1)}, f32[2,128,16,128]{3,2,1,0:T(8,128)}, u32[]{:S(2)}) copy-start(f32[2,128,16,128]{3,2,1,0:T(8,128)} %param.5) | copy-start | bytes 6291460
  51.0 7.7 %copy-start.13 = (s32[8,256]{1,0:T(8,128)S(1)}, s32[8,256]{1,0:T(8,128)}, u32[]{:S(2)}) copy-start(s32[8,256]{1,0:T(8,128)} %param.8) | copy-start | bytes 24580
  51.0 158.2 %all-to-all-start = ((bf16[2,8,128,16,128]{4,3,1,0,2:T(8,128)(2,1)}), bf16[2,8,128,16,128]{4,3,1,0,2:T(8,128)(2,1)}, u32[]{:S(2)}, u32[]{:S(2)}) async-start(bf16[2,8,128,16,128]{4,3,1,0,2:T(8,128)(2,1)} %copy.38), calls=%async_computation | async-start | bytes 16777216 | tf_op jit(solution)/shard_map/all_to_all | solution.py:115
  58.6 491.8 %all-reduce.2.cloned.1.call-start = ((), (), s32[]{:S(2)}) async-start(), calls=%async_computation.2 | async-start | bytes 2097152 | tf_op jit(solution)/shard_map/psum | solution.py:129
  507.4 3.7 copy-start.14
  550.4 1.9 copy-start.12
  556.5 7.4 %copy-start.6 = (f32[2,2,128,16,128]{2,4,3,1,0:T(8,128)}, f32[2,2,128,16,128]{2,4,3,1,0:T(8,128)S(1)}, u32[]{:S(2)}) copy-start(f32[2,2,128,16,128]{2,4,3,1,0:T(8,128)S(1)} %get-tuple-element.15) | copy-start | bytes 12582916
  556.5 7.4 %copy-start.7 = (f32[2,2,128,16,128]{2,4,3,1,0:T(8,128)}, f32[2,2,128,16,128]{2,4,3,1,0:T(8,128)S(1)}, u32[]{:S(2)}) copy-start(f32[2,2,128,16,128]{2,4,3,1,0:T(8,128)S(1)} %get-tuple-element.16) | copy-start | bytes 12582916
  556.6 7.5 %collective-permute-start = (bf16[4,2,128,1,128]{2,4,3,1,0:T(8,128)(2,1)S(1)}, bf16[4,2,128,1,128]{2,4,3,1,0:T(8,128)(2,1)S(1)}, u32[]{:S(2)}, u32[]{:S(2)}) collective-permute-start(bf16[4,2,128,1,128]{2,4,3,1,0:T(8,128)(2,1)S(1)} %fusion.61), channel_id=1, source_target_pairs={{1,0},{4,1},{5,4},{8,5},{9,8},{12,9},{13,12},{16,13},{17,16},{20,1... | collective-permute-start | bytes 786440 | tf_op jit(solution)/shard_map/ppermute | solution.py:15
  570.9 16.8 %copy-start = (f32[4,2,128,16,128]{2,4,3,1,0:T(8,128)}, f32[4,2,128,16,128]{2,4,3,1,0:T(8,128)S(1)}, u32[]{:S(2)}) copy-start(f32[4,2,128,16,128]{2,4,3,1,0:T(8,128)S(1)} %get-tuple-element.12) | copy-start | bytes 25165828
  570.9 16.8 %copy-start.3 = (f32[4,2,128,16,128]{2,4,3,1,0:T(8,128)}, f32[4,2,128,16,128]{2,4,3,1,0:T(8,128)S(1)}, u32[]{:S(2)}) copy-start(f32[4,2,128,16,128]{2,4,3,1,0:T(8,128)S(1)} %get-tuple-element.11) | copy-start | bytes 25165828
  582.9 10.1 %copy-start.4 = (f32[2,2,128,16,128]{2,4,3,1,0:T(8,128)}, f32[2,2,128,16,128]{2,4,3,1,0:T(8,128)S(1)}, u32[]{:S(2)}) copy-start(f32[2,2,128,16,128]{2,4,3,1,0:T(8,128)S(1)} %get-tuple-element.13) | copy-start | bytes 12582916
  582.9 10.1 %copy-start.5 = (f32[2,2,128,16,128]{2,4,3,1,0:T(8,128)}, f32[2,2,128,16,128]{2,4,3,1,0:T(8,128)S(1)}, u32[]{:S(2)}) copy-start(f32[2,2,128,16,128]{2,4,3,1,0:T(8,128)S(1)} %get-tuple-element.14) | copy-start | bytes 12582916
  583.0 13.2 %collective-permute-start.1 = (bf16[4,2,128,2,128]{2,4,3,1,0:T(8,128)(2,1)S(1)}, bf16[4,2,128,2,128]{2,4,3,1,0:T(8,128)(2,1)S(1)}, u32[]{:S(2)}, u32[]{:S(2)}) collective-permute-start(bf16[4,2,128,2,128]{2,4,3,1,0:T(8,128)(2,1)S(1)} %fusion.54), channel_id=1, source_target_pairs={{1,0},{4,1},{5,4},{8,5},{9,8},{12,9},{13,12},{16,13},{17,16},{20,1... | collective-permute-start | bytes 1572872 | tf_op jit(solution)/shard_map/ppermute | solution.py:15
  605.2 3.2 copy-start.1
  608.4 21.4 %slice-start.4 = ((s8[8388608]{0:T(1024)(128)(4,1)}), s8[4194304]{0:T(1024)(128)(4,1)S(1)}, s32[]{:S(2)}) async-start(s8[8388608]{0:T(1024)(128)(4,1)} %bitcast.164), calls=%async_computation.7 | async-start | bytes 8388608
  616.2 13.6 %slice-start.5 = ((s8[8388608]{0:T(1024)(128)(4,1)}), s8[4194304]{0:T(1024)(128)(4,1)S(1)}, s32[]{:S(2)}) async-start(s8[8388608]{0:T(1024)(128)(4,1)} %bitcast.164), calls=%async_computation.8 | async-start | bytes 8388608
  629.7 18.5 %collective-permute-start.2 = (bf16[4,2,128,2,128]{2,4,3,1,0:T(8,128)(2,1)S(1)}, bf16[4,2,128,2,128]{2,4,3,1,0:T(8,128)(2,1)S(1)}, u32[]{:S(2)}, u32[]{:S(2)}) collective-permute-start(bf16[4,2,128,2,128]{2,4,3,1,0:T(8,128)(2,1)S(1)} %slice.450), channel_id=1, source_target_pairs={{29,0},{0,1},{1,4},{4,5},{5,8},{8,9},{9,12},{12,13},{13,16},{16,17... | collective-permute-start | bytes 1572872 | tf_op jit(solution)/shard_map/ppermute | solution.py:15
  659.4 3.2 copy-start.8
  662.7 15.5 %slice-start = ((s8[14680064]{0:T(1024)(128)(4,1)}), s8[4194304]{0:T(1024)(128)(4,1)S(1)}, s32[]{:S(2)}) async-start(s8[14680064]{0:T(1024)(128)(4,1)} %bitcast.162), calls=%async_computation.3 | async-start | bytes 8388608
  662.7 15.5 %slice-start.1 = ((s8[14680064]{0:T(1024)(128)(4,1)}), s8[4194304]{0:T(1024)(128)(4,1)S(1)}, s32[]{:S(2)}) async-start(s8[14680064]{0:T(1024)(128)(4,1)} %bitcast.162), calls=%async_computation.4 | async-start | bytes 8388608
  662.7 15.6 %slice-start.2 = ((s8[14680064]{0:T(1024)(128)(4,1)}), s8[2097152]{0:T(1024)(128)(4,1)S(1)}, s32[]{:S(2)}) async-start(s8[14680064]{0:T(1024)(128)(4,1)} %bitcast.162), calls=%async_computation.5 | async-start | bytes 4194304
  672.6 5.6 slice-start.3
  680.1 3.3 copy-start.10
  683.4 8.5 %collective-permute-start.3 = (bf16[4,2,128,1,128]{2,4,3,1,0:T(8,128)(2,1)S(1)}, bf16[4,2,128,1,128]{2,4,3,1,0:T(8,128)(2,1)S(1)}, u32[]{:S(2)}, u32[]{:S(2)}) collective-permute-start(bf16[4,2,128,1,128]{2,4,3,1,0:T(8,128)(2,1)S(1)} %slice.451), channel_id=1, source_target_pairs={{29,0},{0,1},{1,4},{4,5},{5,8},{8,9},{9,12},{12,13},{13,16},{16,17... | collective-permute-start | bytes 786440 | tf_op jit(solution)/shard_map/ppermute | solution.py:15
  703.4 4.9 copy-start.2
  714.0 3.4 copy-start.9
Sparse Core Ops, SparseCore 0:
  509.2 41.1 all-reduce.1
where the time goes:
time: 731 us; the launch traced here: 727 us
  blocking collectives  219 us (30%)
  waiting for transfers between devices  188 us (26%)
  other arithmetic  166 us (23%)
  local copies, waits for them, and re-layouts  86.6 us (12%)
  matrix products  37.9 us (5%)
  starting transfers between devices  16 us (2%)
  between operations  14.2 us (2%)
    all_to_all x1, blocking collectives, local(): lax.all_to_all(depth_back, ('slab', 'row'), split_axis=3, concat_axis=2,...  219 us
    all_to_all x1, waiting for transfers between devices, local(): lax.all_to_all(phase_done, ('slab', 'row'), split_axis=2, concat_axis=3,...  147 us
    psum x1, waiting for transfers between devices, local(): lax.psum(partial_value.astype(jnp.bfloat16), 'coil').astype(jnp.float32)  39.3 us
    dot_general x4, matrix products, contract(): return jnp.einsum(form, values, table, preferred_element_type=jnp.float32)  37.9 us
    mul x4, other arithmetic, shrink_detail(): return detail * factor[:, None]  32.8 us
    mul x5, other arithmetic, merge_bands(): return (lower + upper + before(lower - upper, along, offset)) * quarter_root  32.6 us
    mul x3, other arithmetic, split_bands(): (bands - moved) * half_root  19.9 us
    sub x6, other arithmetic, merge_bands(): return (lower + upper + before(lower - upper, along, offset)) * quarter_root  19.6 us
  transfers between devices with their start and end apart: 6, of which 4 were waited for; matrix products, arithmetic and copies ran while one was open for 6% of the time, Pallas kernels for 0%

commit v1 on v0

--- a/solution.py
+++ b/solution.py
@@ -126,7 +126,9 @@
             jnp.sum(sens_wide[0] * readout_back[1] - sens_wide[1] * readout_back[0], axis=0),
         ]
     )
-    gradient = lax.psum(partial_value.astype(jnp.bfloat16), "coil").astype(jnp.float32)
+    gradient = jnp.sum(lax.all_gather(partial_value.astype(jnp.bfloat16), "coil"), axis=0).astype(
+        jnp.float32
+    )
     descent = image - step_size * gradient
     moves = [
         (4, roll_after, roll_before),

time: 731 us -> 709 us (0.970)
  other arithmetic: 166 us -> 147 us
  local copies, waits for them, and re-layouts: 86.6 us -> 73.5 us
  waiting for transfers between devices: 188 us -> 199 us
    psum x1 -> x0, waiting for transfers between devices: 39.3 us -> none  [local(): lax.psum(partial_value.astype(jnp.bfloat16), 'coil').astype(jnp.float32)]
    all_gather x0 -> x1, waiting for transfers between devices: none -> 34.3 us  [local(): lax.all_gather(partial_value.astype(jnp.bfloat16), 'coil')]
    ppermute x4, waiting for transfers between devices: 1.27 us -> 17.2 us  [passed_along(): return lax.ppermute(block, axis, route)]
    slice x2 -> x0, local copies, waits for them, and re-layouts: 14.3 us -> none  [plane_before(): remain = lax.slice_in_dim(values, 0, extent - offset, axis=along)]
    mul x3 -> x4, other arithmetic: 19.9 us -> 20.4 us  [split_bands(): (bands - moved) * half_root]
  transfers between devices with their start and end apart: 6 -> 6, of which waited for: 4 -> 5; matrix products, arithmetic and copies ran while one was open for 6% -> 3% of each run, Pallas kernels for 0% -> 0%
where the time goes in v1:
time: 709 us; the launch traced here: 705 us
  blocking collectives  219 us (31%)
  waiting for transfers between devices  199 us (28%)
  other arithmetic  147 us (21%)
  local copies, waits for them, and re-layouts  73.5 us (10%)
  matrix products  37.8 us (5%)
  starting transfers between devices  15.9 us (2%)
  between operations  14.1 us (2%)
    all_to_all x1, blocking collectives, local(): lax.all_to_all(depth_back, ('slab', 'row'), split_axis=3, concat_axis=2,...  219 us
    all_to_all x1, waiting for transfers between devices, local(): lax.all_to_all(phase_done, ('slab', 'row'), split_axis=2, concat_axis=3,...  147 us
    dot_general x4, matrix products, contract(): return jnp.einsum(form, values, table, preferred_element_type=jnp.float32)  37.8 us
    all_gather x1, waiting for transfers between devices, local(): lax.all_gather(partial_value.astype(jnp.bfloat16), 'coil')  34.3 us
    mul x5, other arithmetic, merge_bands(): return (lower + upper + before(lower - upper, along, offset)) * quarter_root  28.4 us
    mul x4, other arithmetic, shrink_detail(): return detail * factor[:, None]  28.1 us
    mul x4, other arithmetic, split_bands(): (bands - moved) * half_root  20.4 us
    ppermute x4, waiting for transfers between devices, passed_along(): return lax.ppermute(block, axis, route)  17.2 us
  transfers between devices with their start and end apart: 6, of which 5 were waited for; matrix products, arithmetic and copies ran while one was open for 3% of the time, Pallas kernels for 0%

profile of v1, /device:TPU:0, one launch (start us, length us, event | category | flops | bytes accessed | tf_op | source)
XLA Modules:
  0.0 705.4 jit_solution(7943010002101296552)
XLA Ops:
  7.4 11.7 %copy_convert_fusion = f32[2,8,128,16,128]{4,2,0,3,1:T(8,128)} fusion(bf16[2,8,128,16,128]{4,3,2,1,0:T(8,128)(2,1)} %param.6), kind=kLoop, calls=%fused_computation.55 | loop fusion | flops 4194304 | bytes 25165824 | tf_op jit(solution)/shard_map/convert_element_type | solution.py:111
  19.9 9.9 %subtract_convert_fusion = (bf16[1,8,128,16,128]{4,2,0,3,1:T(8,128)(2,1)}, bf16[1,8,128,16,128]{4,2,0,3,1:T(8,128)(2,1)}) fusion(f32[2,8,128,16,128]{4,2,0,3,1:T(8,128)} %copy_convert_fusion, f32[128,16,128]{2,0,1:T(8,128)S(1)} %copy.55, f32[128,16,128]{2,0,1:T(8,128)S(1)} %copy.54), kind=kLoop, calls=%fused_computation.63 | loop fusion | flops 16777216 | bytes 27262976 | tf_op jit(solution)/shard_map/convert.9
  29.8 9.0 %fusion.8 = bf16[2,8,128,16,128]{4,2,3,1,0:T(8,128)(2,1)} fusion(bf16[1,8,128,16,128]{4,2,0,3,1:T(8,128)(2,1)} %get-tuple-element.8, bf16[1,8,128,16,128]{4,2,0,3,1:T(8,128)(2,1)} %get-tuple-element.7, bf16[1,2,128,128]{2,3,1,0:T(8,128)(2,1)S(1)} %get-tuple-element.28, bf16[1,2,128,128]{2,3,1,0:T(8,128)(2,1)S(1)} %get-tuple-element.29), kind=kOutput, calls=%fused_computation.32 | convolution fusion | flops 4320657408 | bytes 16908288 | tf_op jit(solution)/shard_map/tcjzx,stjk->sckzx/dot_general | solution.py:31
  38.9 12.0 %copy.57 = bf16[2,8,128,16,128]{4,3,1,0,2:T(8,128)(2,1)} copy(bf16[2,8,128,16,128]{4,2,3,1,0:T(8,128)(2,1)} %fusion.8) | data formatting | bytes 16777216 | tf_op jit(solution)/shard_map/convert_element_type | solution.py:114
  50.9 7.6 %all-to-all-start = ((bf16[2,8,128,16,128]{4,3,1,0,2:T(8,128)(2,1)}), bf16[2,8,128,16,128]{4,3,1,0,2:T(8,128)(2,1)}, u32[]{:S(2)}, u32[]{:S(2)}) async-start(bf16[2,8,128,16,128]{4,3,1,0,2:T(8,128)(2,1)} %copy.57), calls=%async_computation | async-start | bytes 16777216 | tf_op jit(solution)/shard_map/all_to_all | solution.py:115
  58.6 1.0 multiply_convert_fusion.2
  59.5 1.3 multiply_convert_fusion
  60.8 1.0 negate_convert_fusion
  61.9 147.1 %all-to-all-done = bf16[2,8,128,16,128]{4,3,1,0,2:T(8,128)(2,1)} async-done(((bf16[2,8,128,16,128]{4,3,1,0,2:T(8,128)(2,1)}), bf16[2,8,128,16,128]{4,3,1,0,2:T(8,128)(2,1)}, u32[]{:S(2)}, u32[]{:S(2)}) %all-to-all-start) | async-done | bytes 8388640 | tf_op jit(solution)/shard_map/all_to_all | solution.py:115
  209.1 9.1 %copy.59 = bf16[2,8,8,16,16,128]{5,4,3,2,1,0:T(8,128)(2,1)} copy(bf16[2,8,8,16,16,128]{5,4,1,0,2,3:T(8,128)(2,1)} %bitcast.31) | data formatting | bytes 16777216 | tf_op jit(solution)/shard_map/all_to_all | solution.py:115
  218.2 9.5 %fusion.1 = bf16[2,8,8,256,128]{4,3,2,1,0:T(8,128)(2,1)S(1)} fusion(bf16[2,8,8,256,128]{4,3,2,1,0:T(8,128)(2,1)} %param.7, f32[8,256]{1,0:T(8,128)S(1)} %convert_element_type.159, bf16[2,8,8,256,128]{4,3,2,1,0:T(8,128)(2,1)} %bitcast.167, bf16[1,2,256,256]{2,3,1,0:T(8,128)(2,1)S(1)} %get-tuple-element.24, bf16[1,2,256,256]{2,3,1,0:T(8,128)(2,1)S(1)} %get-tuple-element.25), kind=kOutput, calls=%fused_computation.10 | convolution fusion | flops 4312793088 | bytes 25698304 | tf_op jit(solution)/shard_map/tcyjx,stjk->scykx/dot_general | solution.py:31
  227.7 6.7 fusion.9
  234.4 12.0 %copy.62 = bf16[2,8,8,256,128]{4,2,1,0,3:T(8,128)(2,1)} copy(bf16[2,8,8,256,128]{4,3,2,1,0:T(8,128)(2,1)} %fusion.9) | data formatting | bytes 16777216 | tf_op jit(solution)/shard_map/convert_element_type | solution.py:119
  246.5 218.8 %all_to_all.36 = bf16[2,8,8,256,128]{4,2,1,0,3:T(8,128)(2,1)} all-to-all(bf16[2,8,8,256,128]{4,2,1,0,3:T(8,128)(2,1)} %copy.62), channel_id=1, replica_groups=mesh['groups'=1,'slab'=8,'coil'=2,'row'=2] {'slab','row'}, dimensions={3} | all-to-all | bytes 16777216 | tf_op jit(solution)/shard_map/all_to_all | solution.py:120
  465.3 16.3 %copy.64 = bf16[2,8,16,8,16,128]{5,4,3,2,1,0:T(8,128)(2,1)} copy(bf16[2,8,16,8,16,128]{5,3,1,0,4,2:T(8,128)(2,1)} %bitcast.163) | data formatting | bytes 16777216 | tf_op jit(solution)/shard_map/all_to_all | solution.py:120
  481.6 12.5 %convolution_bitcast_fusion = f32[2,8,128,16,128]{4,2,0,3,1:T(8,128)} fusion(bf16[2,8,128,16,128,1]{4,3,2,1,0,5:T(8,128)(2,1)} %bitcast.162, bf16[1,2,128,128]{2,3,1,0:T(8,128)(2,1)S(1)} %get-tuple-element.30, bf16[1,2,128,128]{2,3,1,0:T(8,128)(2,1)S(1)} %get-tuple-element.27), kind=kOutput, calls=%fused_computation.29 | convolution fusion | flops 4299685888 | bytes 25296896 | tf_op jit(solution)/shard_map/tcyzj,stjk->scyzk/dot_general | solution.py:31
  494.1 13.1 %add_reduce_fusion = (bf16[128,16,128]{2,0,1:T(8,128)(2,1)S(1)}, bf16[128,16,128]{2,0,1:T(8,128)(2,1)S(1)}) fusion(f32[2,8,128,16,128]{4,2,0,3,1:T(8,128)} %convolution_bitcast_fusion, f32[2,8,128,16,128]{4,2,0,3,1:T(8,128)} %copy_convert_fusion), kind=kLoop, calls=%fused_computation.61 | loop fusion | flops 16252928 | bytes 34603008 | tf_op jit(solution)/shard_map/reduce_sum | solution.py:125
  507.9 1.7 copy.69
  509.6 34.3 %all-gather.2.cloned.1.call-done = bf16[2,2,128,16,128]{4,3,2,1,0:T(8,128)(2,1)} async-done(((bf16[1,2,128,16,128]{4,3,2,1,0:T(8,128)(2,1)}), bf16[2,2,128,16,128]{4,3,2,1,0:T(8,128)(2,1)}) %all-gather.2.cloned.1.call-update) | async-done | bytes 2097168 | tf_op jit(solution)/shard_map/all_gather | solution.py:129
  543.9 2.3 reduce_sum.32
  546.2 1.8 fusion.53
  548.0 1.9 slice_bitcast_fusion
  549.9 0.8 copy.70
  550.7 1.0 copy.71
  551.7 3.0 multiply_bitcast_fusion
  555.0 0.8 add_multiply_fusion.3
  555.8 0.4 fusion.59
  556.3 3.6 collective-permute-start
  559.8 4.0 fusion.7
  563.8 2.7 collective-permute-done
  566.5 0.5 convert_element_type.171
  567.1 7.0 subtract_multiply_fusion
  574.3 0.6 slice.265
  574.9 0.8 subtract_multiply_fusion.4
  576.0 0.9 add_multiply_fusion.2
  577.4 4.7 collective-permute-start.1
  582.1 5.2 divide_bitcast_fusion
  587.3 3.6 fusion.6
  591.3 9.6 %subtract_multiply_fusion.1 = (f32[4,2,128,16,128]{4,3,2,1,0:T(8,128)}, f32[4,2,128,16,128]{4,3,2,1,0:T(8,128)S(1)}) fusion(f32[2,2,128,16,128]{4,3,2,1,0:T(8,128)} %copy-done.5, f32[2,2,128,16,128]{4,3,2,1,0:T(8,128)} %copy-done.4, f32[4,2,128,2,128]{4,3,2,1,0:T(2,128)S(1)} %convert_element_type.172, f32[4,2,128,14,128]{4,3,2,1,0:T(8,128)} %fusion.6), kind=kLoop, calls=%fused_computation.57 | loop fusion | flops 12582912 | bytes 33554432 | tf_op jit(solution)/shard_map/mul | solution.py:65
  601.1 8.4 %divide_bitcast_fusion.1 = f32[7,128,16,128]{3,2,1,0:T(8,128)} fusion(f32[4,2,128,16,128]{4,3,2,1,0:T(8,128)} %get-tuple-element.9, f32[4,2,128,16,128]{4,3,2,1,0:T(8,128)S(1)} %get-tuple-element.10, f32[7]{0:T(128)S(1)} %get-tuple-element.31), kind=kLoop, calls=%fused_computation.79 | loop fusion | flops 16515072 | bytes 24117276 | tf_op jit(solution)/shard_map/mul | solution.py:79
  609.4 6.4 fusion.5
  615.9 1.2 slice_subtract_fusion.1
  617.1 4.0 copy-done
  621.1 0.5 slice.451
  621.6 2.8 copy-done.8
  624.4 8.1 %fusion.3 = f32[7,2,128,16,128]{4,3,2,1,0:T(8,128)S(1)} fusion(f32[4,2,128,16,128]{4,3,2,1,0:T(8,128)} %copy-done.1, f32[4,2,128,16,128]{4,3,2,1,0:T(8,128)} %copy-done.2, f32[7,128,16,128]{3,2,1,0:T(8,128)} %divide_bitcast_fusion), kind=kLoop, calls=%fused_computation.16 | loop fusion | flops 7340032 | bytes 38797312 | tf_op jit(solution)/shard_map/mul | solution.py:79
  632.5 3.2 collective-permute-done.2
  636.1 12.8 %fusion.12 = f32[4,2,128,16,128]{4,3,2,1,0:T(8,128)} fusion(f32[4,2,128,14,128]{4,3,2,1,0:T(8,128)} %bitcast.160, f32[4,2,128,2,128]{4,3,2,1,0:T(2,128)S(1)} %convert_element_type.173, f32[7,2,128,16,128]{4,3,2,1,0:T(8,128)} %copy-done, f32[1,2,128,16,128]{4,3,2,1,0:T(8,128)} %copy-done.11), kind=kLoop, calls=%fused_computation.42 | loop fusion | flops 10485760 | bytes 42991616 | tf_op jit(solution)/shard_map/mul | solution.py:72
  648.9 4.0 slice_subtract_fusion.3
  652.9 2.4 slice.286
  655.2 5.5 fusion.40
  661.0 0.6 slice.289
  661.6 1.9 fusion.48
  663.5 2.3 slice_subtract_fusion
  665.9 3.3 copy-done.9
  669.1 0.5 slice.452
  669.7 11.3 %collective-permute-done.3 = bf16[4,2,128,1,128]{4,3,2,1,0:T(2,128)(2,1)S(1)} collective-permute-done((bf16[4,2,128,1,128]{4,3,2,1,0:T(2,128)(2,1)S(1)}, bf16[4,2,128,1,128]{4,3,2,1,0:T(2,128)(2,1)S(1)}, u32[]{:S(2)}, u32[]{:S(2)}) %collective-permute-start.3) | collective-permute-done | bytes 262176 | tf_op jit(solution)/shard_map/ppermute | solution.py:15
  681.0 0.5 convert_element_type.174
  681.6 7.3 %fusion.13 = f32[4,2,128,16,128]{4,3,2,1,0:T(8,128)} fusion(f32[4,2,128,15,128]{4,3,2,1,0:T(8,128)} %bitcast.161, f32[4,2,128,1,128]{4,3,2,1,0:T(1,128)S(1)} %convert_element_type.174, f32[7,2,128,16,128]{4,3,2,1,0:T(8,128)S(1)} %fusion.3, f32[1,2,128,16,128]{4,3,2,1,0:T(8,128)} %fusion.48), kind=kLoop, calls=%fused_computation.44 | loop fusion | flops 10485760 | bytes 41943040 | tf_op jit(solution)/shard_map/mul | solution.py:72
  688.9 4.2 slice_subtract_fusion.2
  693.4 1.3 copy-done.3
  694.7 0.8 fusion.41
  695.8 0.6 slice.304
  696.4 1.9 fusion.50
  (56 shorter events, 5.6 us)
Async XLA Ops:
  7.4 11.7 %copy-start.10 = (f32[2,128,16,128]{3,2,1,0:T(8,128)S(1)}, f32[2,128,16,128]{3,2,1,0:T(8,128)}, u32[]{:S(2)}) copy-start(f32[2,128,16,128]{3,2,1,0:T(8,128)} %param.5) | copy-start | bytes 6291460
  50.9 7.7 %copy-start.12 = (s32[8,256]{1,0:T(8,128)S(1)}, s32[8,256]{1,0:T(8,128)}, u32[]{:S(2)}) copy-start(s32[8,256]{1,0:T(8,128)} %param.8) | copy-start | bytes 24580
  50.9 158.2 %all-to-all-start = ((bf16[2,8,128,16,128]{4,3,1,0,2:T(8,128)(2,1)}), bf16[2,8,128,16,128]{4,3,1,0,2:T(8,128)(2,1)}, u32[]{:S(2)}, u32[]{:S(2)}) async-start(bf16[2,8,128,16,128]{4,3,1,0,2:T(8,128)(2,1)} %copy.57), calls=%async_computation | async-start | bytes 16777216 | tf_op jit(solution)/shard_map/all_to_all | solution.py:115
  58.5 485.4 %all-gather.2.cloned.1.call-start = ((), (), s32[]{:S(2)}) async-start(), calls=%async_computation.2 | async-start | bytes 3145728 | tf_op jit(solution)/shard_map/all_gather | solution.py:129
  507.2 2.4 copy-start.13
  555.8 8.0 %copy-start.6 = (f32[2,2,128,16,128]{4,3,2,1,0:T(8,128)}, f32[2,2,128,16,128]{4,3,2,1,0:T(8,128)S(1)}, u32[]{:S(2)}) copy-start(f32[2,2,128,16,128]{4,3,2,1,0:T(8,128)S(1)} %get-tuple-element.17) | copy-start | bytes 12582916
  555.8 8.0 %copy-start.7 = (f32[2,2,128,16,128]{4,3,2,1,0:T(8,128)}, f32[2,2,128,16,128]{4,3,2,1,0:T(8,128)S(1)}, u32[]{:S(2)}) copy-start(f32[2,2,128,16,128]{4,3,2,1,0:T(8,128)S(1)} %get-tuple-element.18) | copy-start | bytes 12582916
  556.3 10.3 %collective-permute-start = (bf16[4,2,128,1,128]{4,3,2,1,0:T(2,128)(2,1)S(1)}, bf16[4,2,128,1,128]{4,3,2,1,0:T(2,128)(2,1)S(1)}, u32[]{:S(2)}, u32[]{:S(2)}) collective-permute-start(bf16[4,2,128,1,128]{4,3,2,1,0:T(2,128)(2,1)S(1)} %fusion.59), channel_id=1, source_target_pairs={{1,0},{4,1},{5,4},{8,5},{9,8},{12,9},{13,12},{16,13},{17,16},{20,1... | collective-permute-start | bytes 786440 | tf_op jit(solution)/shard_map/ppermute | solution.py:15
  574.1 8.0 %copy-start.1 = (f32[4,2,128,16,128]{4,3,2,1,0:T(8,128)}, f32[4,2,128,16,128]{4,3,2,1,0:T(8,128)S(1)}, u32[]{:S(2)}) copy-start(f32[4,2,128,16,128]{4,3,2,1,0:T(8,128)S(1)} %get-tuple-element.12) | copy-start | bytes 25165828
  574.1 8.0 %copy-start.2 = (f32[4,2,128,16,128]{4,3,2,1,0:T(8,128)}, f32[4,2,128,16,128]{4,3,2,1,0:T(8,128)S(1)}, u32[]{:S(2)}) copy-start(f32[4,2,128,16,128]{4,3,2,1,0:T(8,128)S(1)} %get-tuple-element.11) | copy-start | bytes 25165828
  576.9 10.4 %copy-start.4 = (f32[2,2,128,16,128]{4,3,2,1,0:T(8,128)}, f32[2,2,128,16,128]{4,3,2,1,0:T(8,128)S(1)}, u32[]{:S(2)}) copy-start(f32[2,2,128,16,128]{4,3,2,1,0:T(8,128)S(1)} %get-tuple-element.15) | copy-start | bytes 12582916
  577.0 10.4 %copy-start.5 = (f32[2,2,128,16,128]{4,3,2,1,0:T(8,128)}, f32[2,2,128,16,128]{4,3,2,1,0:T(8,128)S(1)}, u32[]{:S(2)}) copy-start(f32[2,2,128,16,128]{4,3,2,1,0:T(8,128)S(1)} %get-tuple-element.16) | copy-start | bytes 12582916
  577.4 13.6 %collective-permute-start.1 = (bf16[4,2,128,2,128]{4,3,2,1,0:T(2,128)(2,1)S(1)}, bf16[4,2,128,2,128]{4,3,2,1,0:T(2,128)(2,1)S(1)}, u32[]{:S(2)}, u32[]{:S(2)}) collective-permute-start(bf16[4,2,128,2,128]{4,3,2,1,0:T(2,128)(2,1)S(1)} %fusion.52), channel_id=1, source_target_pairs={{1,0},{4,1},{5,4},{8,5},{9,8},{12,9},{13,12},{16,13},{17,16},{20,1... | collective-permute-start | bytes 1572872 | tf_op jit(solution)/shard_map/ppermute | solution.py:15
  601.1 14.8 %copy-start.11 = (f32[1,2,128,16,128]{4,3,2,1,0:T(8,128)}, f32[1,2,128,16,128]{4,3,2,1,0:T(8,128)S(1)}, u32[]{:S(2)}) copy-start(f32[1,2,128,16,128]{4,3,2,1,0:T(8,128)S(1)} %slice.275) | copy-start | bytes 6291460
  615.9 5.2 copy-start
  621.1 3.3 copy-start.8
  624.4 11.3 %collective-permute-start.2 = (bf16[4,2,128,2,128]{4,3,2,1,0:T(2,128)(2,1)S(1)}, bf16[4,2,128,2,128]{4,3,2,1,0:T(2,128)(2,1)S(1)}, u32[]{:S(2)}, u32[]{:S(2)}) collective-permute-start(bf16[4,2,128,2,128]{4,3,2,1,0:T(2,128)(2,1)S(1)} %slice.451), channel_id=1, source_target_pairs={{29,0},{0,1},{1,4},{4,5},{5,8},{8,9},{9,12},{12,13},{13,16},{16,17... | collective-permute-start | bytes 1572872 | tf_op jit(solution)/shard_map/ppermute | solution.py:15
  665.9 3.3 copy-start.9
  669.7 11.4 %collective-permute-start.3 = (bf16[4,2,128,1,128]{4,3,2,1,0:T(2,128)(2,1)S(1)}, bf16[4,2,128,1,128]{4,3,2,1,0:T(2,128)(2,1)S(1)}, u32[]{:S(2)}, u32[]{:S(2)}) collective-permute-start(bf16[4,2,128,1,128]{4,3,2,1,0:T(2,128)(2,1)S(1)} %slice.452), channel_id=1, source_target_pairs={{29,0},{0,1},{1,4},{4,5},{5,8},{8,9},{9,12},{12,13},{13,16},{16,17... | collective-permute-start | bytes 786440 | tf_op jit(solution)/shard_map/ppermute | solution.py:15
  688.9 5.8 copy-start.3
Sparse Core Ops, SparseCore 0:
  509.7 34.1 all-gather.1
